TPU v7x, 256 devices: a whole 4x4x8 slice. The times are simulated.
256 devices in a mesh: dp: 32 (over x_hi, z, core), tensor: 8 (over y, x_lo).
Axes of the slice: x: 4 (x_hi: 2, x_lo: 2; x = x_hi * 2 + x_lo), y: 4, z: 8, core: 2. Of those that a mesh axis runs over, the one named last changes fastest.
Arguments:
- grad_hidden: bfloat16 [4096, 14336], P('dp', 'tensor'), may hold values from -18 to 18
- gate: bfloat16 [4096, 14336], P('dp', 'tensor'), may hold values from -6 to 6
Outputs:
- factor: float32 [14336, 14336], P('tensor', 'dp')
All inputs are finite; a program needn't handle non-finite values.
Results may differ from a plain program's by a relative error of at most 0.0065.
Values may be sent and summed in bfloat16 or wider, within the bound.
A program may use at most 128 MiB of HBM per device.

v0:
```python
import jax
import jax.numpy as jnp
from jax import lax
from jax.sharding import PartitionSpec as P

FF = 14336


def broadcast(block, axis, owner):
    block = jnp.where(lax.axis_index(axis) == owner, block, jnp.zeros_like(block))
    return lax.psum(block, axis)


def shards(grad_hidden, gate):
    up_grad = (grad_hidden.astype(jnp.float32) * jax.nn.silu(gate.astype(jnp.float32))).astype(
        jnp.bfloat16
    )
    tensor_count = lax.axis_size("tensor")
    data_count = lax.axis_size("dp")
    col_width = FF // data_count
    ratio = data_count // tensor_count
    data_index = lax.axis_index("dp")
    owner = data_index // ratio
    offset = data_index % ratio * col_width
    contract = (((0,), (0,)), ((), ()))
    total_tokens = up_grad.shape[0] * data_count
    rows_all = lax.all_gather(up_grad, "dp", axis=0, tiled=True)
    panel = lax.dynamic_slice_in_dim(rows_all, offset, col_width, 1)
    cols_all = broadcast(panel, "tensor", owner)
    summed = lax.dot_general(rows_all, cols_all, contract, preferred_element_type=jnp.float32)
    return summed / total_tokens


def solution(mesh):
    return jax.shard_map(
        shards,
        mesh=mesh,
        in_specs=(P("dp", "tensor"), P("dp", "tensor")),
        out_specs=P("tensor", "dp"),
        check_vma=False,
    )
```

profile of v0, /device:TPU:1, one launch (start us, length us, event | category | flops | bytes accessed | tf_op | source)
XLA Modules:
  0.0 352.8 jit_solution(12489471338623991828)
XLA Ops:
  6.5 0.0 all-gather.2.cloned.1.call-start
  6.5 2.2 fusion.4
  8.7 0.0 all-gather.2.cloned.1.call-update
  8.8 0.0 all-reduce.2.cloned.1.call-start
  8.8 132.4 %all-gather.2.cloned.1.call-done = bf16[4096,1792]{1,0:T(8,128)(2,1)} async-done(((bf16[128,1792]{1,0:T(8,128)(2,1)}), bf16[4096,1792]{1,0:T(8,128)(2,1)}) %all-gather.2.cloned.1.call-update) | async-done | bytes 14680080 | tf_op jit(solution)/shard_map/all_gather | solution.py:27
  141.3 7.3 %dynamic-slice_select_fusion = bf16[4096,448]{1,0:T(8,128)(2,1)} fusion(bf16[4096,1792]{1,0:T(8,128)(2,1)} %all-gather.2.cloned.1.call-done, s32[]{:T(128)S(6)} %select_n.25, pred[]{:T(512)S(6)} %eq.5), kind=kLoop, calls=%fused_computation | loop fusion | flops 1835008 | bytes 7340037 | tf_op jit(solution)/shard_map/jit(_where)/select_n | solution.py:10
  148.6 0.0 all-reduce.2.cloned.1.call-update
  148.6 184.0 %all-reduce.2.cloned.1.call-done = bf16[4096,448]{1,0:T(8,128)(2,1)} async-done(((bf16[4096,448]{1,0:T(8,128)(2,1)}), bf16[4096,448]{1,0:T(8,128)(2,1)}) %all-reduce.2.cloned.1.call-update) | async-done | bytes 3670032 | tf_op jit(solution)/shard_map/psum | solution.py:11
  332.6 13.4 %convolution_multiply_fusion = f32[1792,448]{0,1:T(8,128)} fusion(bf16[4096,1792]{1,0:T(8,128)(2,1)} %all-gather.2.cloned.1.call-done, bf16[4096,448]{1,0:T(8,128)(2,1)} %all-reduce.2.cloned.1.call-done), kind=kOutput, calls=%fused_computation.1 | convolution fusion | flops 6577471488 | bytes 21561344 | tf_op jit(solution)/shard_map/dot_general | solution.py:30
Async XLA Ops:
  6.5 134.7 %all-gather.2.cloned.1.call-start = ((), (), s32[]{:S(2)}) async-start(), calls=%async_computation | async-start | bytes 15138816 | tf_op jit(solution)/shard_map/all_gather | solution.py:27
  8.8 323.8 %all-reduce.2.cloned.1.call-start = ((), (), s32[]{:S(2)}) async-start(), calls=%async_computation.1 | async-start | bytes 8388608 | tf_op jit(solution)/shard_map/psum | solution.py:11
Sparse Core Ops, SparseCore 0:
  10.1 131.1 all-gather.1
  148.7 183.7 all-reduce.1
where the time goes:
time: 353 us
  waiting for transfers between devices  316 us (90%)
  matrix products  13.4 us (4%)
  between operations  13.4 us (4%)
  other arithmetic  9.53 us (3%)
    psum x1, waiting for transfers between devices, broadcast(): return lax.psum(block, axis)  184 us
    all_gather x1, waiting for transfers between devices, shards(): rows_all = lax.all_gather(up_grad, 'dp', axis=0, tiled=True)  132 us
    dot_general x1, matrix products, shards(): lax.dot_general(rows_all, cols_all, contract, preferred_element_type=jnp....  13.4 us
    select_n x1, other arithmetic, broadcast(): jnp.where(lax.axis_index(axis) == owner, block, jnp.zeros_like(block))  7.33 us
  transfers between devices with their start and end apart: 2, of which 2 were waited for; matrix products, arithmetic and copies ran while one was open for 0% of the time, Pallas kernels for 0%

commit v1 on v0

--- a/solution.py
+++ b/solution.py
@@ -24,7 +24,8 @@
     offset = data_index % ratio * col_width
     contract = (((0,), (0,)), ((), ()))
     total_tokens = up_grad.shape[0] * data_count
-    rows_all = lax.all_gather(up_grad, "dp", axis=0, tiled=True)
+    sent = jnp.stack([up_grad] * lax.axis_size("dp"))
+    rows_all = jnp.concatenate(lax.all_to_all(sent, "dp", 0, 0), axis=0)
     panel = lax.dynamic_slice_in_dim(rows_all, offset, col_width, 1)
     cols_all = broadcast(panel, "tensor", owner)
     summed = lax.dot_general(rows_all, cols_all, contract, preferred_element_type=jnp.float32)

time: 353 us -> 567 us (1.61)
  waiting for transfers between devices: 316 us -> 512 us
  starting transfers between devices: 0.04 us -> 12.7 us
  local copies, waits for them, and re-layouts: 0 us -> 6.85 us
    all_to_all x0 -> x1, waiting for transfers between devices: none -> 318 us  [shards(): rows_all = jnp.concatenate(lax.all_to_all(sent, 'dp', 0, 0), axis=0)]
    all_gather x1 -> x0, waiting for transfers between devices: 132 us -> none  [shards(): rows_all = lax.all_gather(up_grad, 'dp', axis=0, tiled=True)]
    all_to_all x0 -> x1, starting transfers between devices: none -> 12.6 us  [shards(): rows_all = jnp.concatenate(lax.all_to_all(sent, 'dp', 0, 0), axis=0)]
    psum x1, waiting for transfers between devices: 184 us -> 193 us  [broadcast(): return lax.psum(block, axis)]
    another operation x0 -> x1, local copies, waits for them, and re-layouts: none -> 6.85 us  [shards(): sent = jnp.stack([up_grad] * lax.axis_size('dp'))]
where the time goes in v1:
time: 567 us
  waiting for transfers between devices  512 us (90%)
  matrix products  13.4 us (2%)
  between operations  13.4 us (2%)
  starting transfers between devices  12.7 us (2%)
  other arithmetic  8.77 us (2%)
  local copies, waits for them, and re-layouts  6.85 us (1%)
    all_to_all x1, waiting for transfers between devices, shards(): rows_all = jnp.concatenate(lax.all_to_all(sent, 'dp', 0, 0), axis=0)  318 us
    psum x1, waiting for transfers between devices, broadcast(): return lax.psum(block, axis)  193 us
    dot_general x1, matrix products, shards(): lax.dot_general(rows_all, cols_all, contract, preferred_element_type=jnp....  13.4 us
    all_to_all x1, starting transfers between devices, shards(): rows_all = jnp.concatenate(lax.all_to_all(sent, 'dp', 0, 0), axis=0)  12.6 us
  transfers between devices with their start and end apart: 2, of which 2 were waited for; matrix products, arithmetic and copies ran while one was open for 0% of the time, Pallas kernels for 0%

profile of v1, /device:TPU:1, one launch (start us, length us, event | category | flops | bytes accessed | tf_op | source)
XLA Modules:
  0.0 567.1 jit_solution(14314838638314270907)
XLA Ops:
  6.5 1.4 fusion.4
  8.0 6.8 %stack.2 = bf16[32,128,1792]{2,1,0:T(8,128)(2,1)} broadcast(bf16[128,1792]{1,0:T(8,128)(2,1)S(1)} %fusion.4), dimensions={1,2} | broadcast | bytes 15138816 | tf_op jit(solution)/shard_map/stack | solution.py:27
  14.8 12.6 %all-to-all-start = ((bf16[32,128,1792]{2,1,0:T(8,128)(2,1)}), bf16[32,128,1792]{2,1,0:T(8,128)(2,1)}, u32[]{:S(2)}, u32[]{:S(2)}) async-start(bf16[32,128,1792]{2,1,0:T(8,128)(2,1)} %stack.2), calls=%async_computation | async-start | bytes 29360128 | tf_op jit(solution)/shard_map/all_to_all | solution.py:28
  27.5 0.0 all-reduce.2.cloned.1.call-start
  27.5 318.5 %all-to-all-done = bf16[32,128,1792]{2,1,0:T(8,128)(2,1)} async-done(((bf16[32,128,1792]{2,1,0:T(8,128)(2,1)}), bf16[32,128,1792]{2,1,0:T(8,128)(2,1)}, u32[]{:S(2)}, u32[]{:S(2)}) %all-to-all-start) | async-done | bytes 14680096 | tf_op jit(solution)/shard_map/all_to_all | solution.py:28
  346.0 7.3 %dynamic-slice_select_fusion = bf16[4096,448]{1,0:T(8,128)(2,1)} fusion(bf16[4096,1792]{1,0:T(8,128)(2,1)} %bitcast, s32[]{:T(128)S(6)} %select_n.25, pred[]{:T(512)S(6)} %eq.5), kind=kLoop, calls=%fused_computation | loop fusion | flops 1835008 | bytes 7340037 | tf_op jit(solution)/shard_map/jit(_where)/select_n | solution.py:10
  353.4 0.0 all-reduce.2.cloned.1.call-update
  353.4 193.4 %all-reduce.2.cloned.1.call-done = bf16[4096,448]{1,0:T(8,128)(2,1)} async-done(((bf16[4096,448]{1,0:T(8,128)(2,1)}), bf16[4096,448]{1,0:T(8,128)(2,1)}) %all-reduce.2.cloned.1.call-update) | async-done | bytes 3670032 | tf_op jit(solution)/shard_map/psum | solution.py:11
  546.8 13.4 %convolution_multiply_fusion = f32[1792,448]{0,1:T(8,128)} fusion(bf16[4096,1792]{1,0:T(8,128)(2,1)} %bitcast, bf16[4096,448]{1,0:T(8,128)(2,1)} %all-reduce.2.cloned.1.call-done), kind=kOutput, calls=%fused_computation.1 | convolution fusion | flops 6577471488 | bytes 21561344 | tf_op jit(solution)/shard_map/dot_general | solution.py:31
Async XLA Ops:
  14.8 331.2 %all-to-all-start = ((bf16[32,128,1792]{2,1,0:T(8,128)(2,1)}), bf16[32,128,1792]{2,1,0:T(8,128)(2,1)}, u32[]{:S(2)}, u32[]{:S(2)}) async-start(bf16[32,128,1792]{2,1,0:T(8,128)(2,1)} %stack.2), calls=%async_computation | async-start | bytes 29360128 | tf_op jit(solution)/shard_map/all_to_all | solution.py:28
  27.5 519.4 %all-reduce.2.cloned.1.call-start = ((), (), s32[]{:S(2)}) async-start(), calls=%async_computation.1 | async-start | bytes 8388608 | tf_op jit(solution)/shard_map/psum | solution.py:11
Sparse Core Ops, SparseCore 0:
  353.5 193.2 all-reduce.1
